TPU v7x, 128 devices: a whole 4x4x4 slice. The times are simulated.
128 devices in a mesh: dp: 1, ep2: 2 (over core), ep: 64 (over z, y, x).
Axes of the slice: x: 4, y: 4, z: 4, core: 2. Of those that a mesh axis runs over, the one named last changes fastest.
Arguments:
- tokens: bfloat16 [16384, 2048], P(('dp', 'ep2', 'ep'))
- expert_idx: int32 [16384, 8], P(('dp', 'ep2', 'ep'))
- gates: float32 [16384, 8], P(('dp', 'ep2', 'ep'))
- w_gate: bfloat16 [128, 2048, 768], P(('ep2', 'ep'))
- w_up: bfloat16 [128, 2048, 768], P(('ep2', 'ep'))
- w_down: bfloat16 [128, 768, 2048], P(('ep2', 'ep'))
Outputs:
- output: bfloat16 [16384, 2048], P(('dp', 'ep2', 'ep'))
All inputs are finite; a program needn't handle non-finite values.
Results may differ from a plain program's by a relative error of at most 0.00119.
Values are sent between devices in bfloat16 or wider.
A program may use at most 1 GiB of HBM per device.

v0:
```python
import jax
import jax.numpy as jnp
from jax import lax
from jax.sharding import PartitionSpec as P


def solution(mesh):
    n_outer = mesh.shape['ep2']
    n_inner = mesh.shape['ep']
    row_spec = P(('dp', 'ep2', 'ep'), None)
    weight_spec = P(('ep2', 'ep'), None, None)

    def local_step(tokens, expert_idx, gates, w_gate, w_up, w_down):
        tok_rows, d_model = tokens.shape
        top_k = expert_idx.shape[1]
        local_exp = w_gate.shape[0]
        n_experts = local_exp * n_outer * n_inner
        capacity = (tok_rows * top_k + n_experts - 1) // n_experts
        n_slots = n_experts * capacity
        flat_ids = expert_idx.reshape(-1)
        one_hot = (flat_ids[:, None] == jnp.arange(n_experts, dtype=jnp.int32)[None, :]).astype(jnp.int32)
        slot_rank = jnp.sum((jnp.cumsum(one_hot, axis=0) - 1) * one_hot, axis=1)
        slot_ids = flat_ids * capacity + slot_rank
        token_of = jnp.arange(tok_rows * top_k, dtype=jnp.int32) // top_k
        source_row = jax.ops.segment_sum(token_of - tok_rows, slot_ids, num_segments=n_slots) + tok_rows
        send_buf = jnp.take(tokens, source_row, axis=0, mode='fill', fill_value=0)
        send_buf = send_buf.reshape(n_outer, n_inner, local_exp, capacity, d_model)
        received = lax.all_to_all(send_buf, 'ep', 1, 1, tiled=True)
        received = lax.all_to_all(received, 'ep2', 0, 0, tiled=True)
        act_gate = jnp.einsum('abecd,edf->abecf', received, w_gate, preferred_element_type=jnp.float32)
        act_up = jnp.einsum('abecd,edf->abecf', received, w_up, preferred_element_type=jnp.float32)
        inner_act = (jax.nn.silu(act_gate) * act_up).astype(jnp.bfloat16)
        expert_out = jnp.einsum('abecf,efd->abecd', inner_act, w_down, preferred_element_type=jnp.float32).astype(jnp.bfloat16)
        returned = lax.all_to_all(expert_out, 'ep2', 0, 0, tiled=True)
        returned = lax.all_to_all(returned, 'ep', 1, 1, tiled=True)
        routed = jnp.take(returned.reshape(n_slots, d_model), slot_ids, axis=0).reshape(tok_rows, top_k, d_model)
        mixed = jnp.sum(gates[:, :, None] * routed, axis=1)
        return (tokens + mixed).astype(jnp.bfloat16)

    return jax.shard_map(local_step, mesh=mesh, in_specs=(row_spec, row_spec, row_spec, weight_spec, weight_spec, weight_spec), out_specs=row_spec, check_vma=False)
```

profile of v0, /device:TPU:1, one launch (start us, length us, event | category | flops | bytes accessed | tf_op | source)
XLA Modules:
  0.0 228.7 jit_solution(3518430634226566430)
XLA Ops:
  0.0 0.0 copy-start
  0.0 0.9 copy.28
  0.9 0.1 eq.26
  1.0 0.1 reshape.119
  1.1 0.7 broadcast_multiply_fusion
  1.8 0.1 copy.30
  1.9 0.2 fusion.25
  2.1 0.0 copy-start.3
  2.1 0.8 copy-done.3
  3.0 1.1 add_add_fusion
  4.0 0.9 copy.31
  4.9 0.1 copy.34
  5.0 0.1 mul.45
  5.1 1.4 fusion.24
  6.6 7.6 %scatter_custom_fusion = s32[1024]{0:T(1024)S(1)} fusion(s32[1024]{0:T(1024)S(1)} %bitcast.103, s32[1024]{0:T(1024)S(1)} %fusion.28, s32[]{:T(128)} %constant.56.clone.1), kind=kCustom, calls=%fused_computation.47 | custom fusion | flops 1024 | bytes 4100 | tf_op jit(solution)/shard_map/scatter-add | solution.py:25
  14.2 0.1 broadcast_in_dim.29
  14.3 9.9 %gather_fusion = bf16[1024,2048]{1,0:T(8,128)(2,1)} fusion(bf16[128,2048]{1,0:T(8,128)(2,1)} %param.6, s32[1024]{0:T(1024)S(1)} %fusion.32), kind=kCustom, calls=%fused_computation | custom fusion | bytes 8392704 | tf_op jit(solution)/shard_map/jit(_take)/gather | solution.py:26
  24.3 2.5 %copy_select_fusion = bf16[2,64,1,8,2048]{4,3,0,2,1:T(8,128)(2,1)S(1)} fusion(bf16[2,64,1,8,2048]{4,3,1,0,2:T(8,128)(2,1)} %bitcast.100, pred[2,64,8]{2,0,1:T(4,128)(4,1)S(1)} %copy.35), kind=kLoop, calls=%fused_computation.9 | loop fusion | flops 2097152 | bytes 8389632 | tf_op jit(solution)/shard_map/jit(_take)/select_n | solution.py:26
  26.8 71.4 %all_to_all.20 = bf16[2,64,1,8,2048]{4,3,0,2,1:T(8,128)(2,1)S(1)} all-to-all(bf16[2,64,1,8,2048]{4,3,0,2,1:T(8,128)(2,1)S(1)} %copy_select_fusion), channel_id=1, replica_groups=mesh['dp'=1,'ep2'=2,'ep'=64] {'ep'}, dimensions={1} | all-to-all | bytes 8388608 | tf_op jit(solution)/shard_map/all_to_all | solution.py:28
  98.2 0.6 copy.37
  98.8 0.0 copy-start.6
  98.8 7.0 %all_to_all.21 = bf16[2,64,1,8,2048]{4,3,1,2,0:T(8,128)(2,1)S(1)} all-to-all(bf16[2,64,1,8,2048]{4,3,1,2,0:T(8,128)(2,1)S(1)} %copy.37), channel_id=1, replica_groups=mesh['dp'=1,'ep2'=2,'ep'=64] {'ep2'}, dimensions={0} | all-to-all | bytes 8388608 | tf_op jit(solution)/shard_map/all_to_all | solution.py:29
  105.8 0.0 copy-start.2
  105.8 1.9 copy-done.2
  107.7 0.0 copy-done.6
  107.7 5.2 %fusion = f32[2,64,8,768]{3,2,1,0:T(8,128)} fusion(bf16[2,64,1,8,2048]{4,3,1,2,0:T(8,128)(2,1)S(1)} %all_to_all.21, bf16[1,2048,768]{2,1,0:T(8,128)(2,1)S(1)} %copy-done.6), kind=kOutput, calls=%fused_computation.5 | convolution fusion | flops 3221225472 | bytes 10485760 | tf_op jit(solution)/shard_map/abecd,edf->abecf/dot_general | solution.py:31
  112.9 0.0 copy-done
  112.9 12.3 %convert_bitcast_fusion = bf16[2,64,1,8,2048]{4,3,1,2,0:T(8,128)(2,1)} fusion(bf16[1,768,2048]{2,1,0:T(8,128)(2,1)S(1)} %copy-done, f32[2,64,8,768]{3,2,1,0:T(8,128)} %fusion, bf16[1,2048,768]{2,1,0:T(8,128)(2,1)} %param.9, bf16[2,64,1,8,2048]{4,3,1,2,0:T(8,128)(2,1)} %copy-done.2), kind=kOutput, calls=%fused_computation.10 | convolution fusion | flops 6449266688 | bytes 17825792 | tf_op jit(solution)/shard_map/abecf,efd->abecd/dot_general | solution.py:33
  125.2 8.5 %all_to_all.22 = bf16[2,64,1,8,2048]{4,3,1,2,0:T(8,128)(2,1)S(1)} all-to-all(bf16[2,64,1,8,2048]{4,3,1,2,0:T(8,128)(2,1)} %convert_bitcast_fusion), channel_id=1, replica_groups=mesh['dp'=1,'ep2'=2,'ep'=64] {'ep2'}, dimensions={0} | all-to-all | bytes 8388608 | tf_op jit(solution)/shard_map/all_to_all | solution.py:34
  133.7 2.3 copy.39
  136.0 0.0 copy-start.4
  136.0 0.0 copy-start.5
  136.0 8.3 %all-to-all-start.3 = ((bf16[2,64,1,8,2048]{4,3,0,2,1:T(8,128)(2,1)}), bf16[2,64,1,8,2048]{4,3,0,2,1:T(8,128)(2,1)}, u32[]{:S(2)}, u32[]{:S(2)}) async-start(bf16[2,64,1,8,2048]{4,3,0,2,1:T(8,128)(2,1)} %copy.39), calls=%async_computation.3 | async-start | bytes 8388608 | tf_op jit(solution)/shard_map/all_to_all | solution.py:35
  144.3 0.1 reduce_sum.23
  144.5 0.0 copy-done.4
  144.5 0.1 copy.33
  144.6 0.0 copy-done.5
  144.6 0.1 copy.27
  144.8 61.0 %all-to-all-done.3 = bf16[2,64,1,8,2048]{4,3,0,2,1:T(8,128)(2,1)} async-done(((bf16[2,64,1,8,2048]{4,3,0,2,1:T(8,128)(2,1)}), bf16[2,64,1,8,2048]{4,3,0,2,1:T(8,128)(2,1)}, u32[]{:S(2)}, u32[]{:S(2)}) %all-to-all-start.3) | async-done | bytes 4194336 | tf_op jit(solution)/shard_map/all_to_all | solution.py:35
  205.8 4.7 %copy.40 = bf16[2,64,1,8,2048]{4,3,1,0,2:T(8,128)(2,1)} copy(bf16[2,64,1,8,2048]{4,3,0,2,1:T(8,128)(2,1)} %all-to-all-done.3) | data formatting | bytes 8388608 | tf_op jit(solution)/shard_map/all_to_all | solution.py:35
  210.5 11.6 %gather_fusion.1 = bf16[1024,2048]{1,0:T(8,128)(2,1)} fusion(bf16[1024,2048]{1,0:T(8,128)(2,1)} %bitcast.99, s32[1024]{0:T(1024)S(1)} %broadcast_clamp_fusion), kind=kCustom, calls=%fused_computation.1 | custom fusion | bytes 8392704 | tf_op jit(solution)/shard_map/jit(_take)/gather | solution.py:36
  222.1 0.0 copy-start.1
  222.1 5.6 %multiply_reduce_fusion = f32[128,2048]{1,0:T(8,128)S(1)} fusion(bf16[1024,2048]{1,0:T(8,128)(2,1)} %gather_fusion.1, f32[128,8]{1,0:T(8,128)S(1)} %copy.27, pred[128,8]{1,0:T(8,128)(4,1)S(1)} %copy.33), kind=kLoop, calls=%fused_computation.3 | loop fusion | flops 8126464 | bytes 5248000 | tf_op jit(solution)/shard_map/reduce_sum | solution.py:37
  227.8 0.0 copy-done.1
  227.8 0.9 add_convert_fusion
  (11 shorter events, 0.2 us)
Async XLA Ops:
  0.0 112.9 %copy-start = (bf16[1,768,2048]{2,1,0:T(8,128)(2,1)S(1)}, bf16[1,768,2048]{2,1,0:T(8,128)(2,1)}, u32[]{:S(2)}) copy-start(bf16[1,768,2048]{2,1,0:T(8,128)(2,1)} %param.11) | copy-start | bytes 9437188
  2.1 0.8 copy-start.3
  98.8 9.0 %copy-start.6 = (bf16[1,2048,768]{2,1,0:T(8,128)(2,1)S(1)}, bf16[1,2048,768]{2,1,0:T(8,128)(2,1)}, u32[]{:S(2)}) copy-start(bf16[1,2048,768]{2,1,0:T(8,128)(2,1)} %param.10) | copy-start | bytes 9437188
  105.8 1.9 copy-start.2
  136.0 8.5 %copy-start.4 = (s32[128,8]{0,1:T(8,128)S(1)}, s32[128,8]{0,1:T(8,128)}, u32[]{:S(2)}) copy-start(s32[128,8]{0,1:T(8,128)} %param.7) | copy-start | bytes 12292
  136.0 8.7 %copy-start.5 = (f32[128,8]{0,1:T(8,128)S(1)}, f32[128,8]{0,1:T(8,128)}, u32[]{:S(2)}) copy-start(f32[128,8]{0,1:T(8,128)} %param.8) | copy-start | bytes 12292
  136.0 69.8 %all-to-all-start.3 = ((bf16[2,64,1,8,2048]{4,3,0,2,1:T(8,128)(2,1)}), bf16[2,64,1,8,2048]{4,3,0,2,1:T(8,128)(2,1)}, u32[]{:S(2)}, u32[]{:S(2)}) async-start(bf16[2,64,1,8,2048]{4,3,0,2,1:T(8,128)(2,1)} %copy.39), calls=%async_computation.3 | async-start | bytes 8388608 | tf_op jit(solution)/shard_map/all_to_all | solution.py:35
  222.1 5.7 %copy-start.1 = (bf16[128,2048]{1,0:T(8,128)(2,1)S(1)}, bf16[128,2048]{1,0:T(8,128)(2,1)}, u32[]{:S(2)}) copy-start(bf16[128,2048]{1,0:T(8,128)(2,1)} %param.6) | copy-start | bytes 1572868
where the time goes:
time: 229 us
  blocking collectives  86.9 us (38%)
  waiting for transfers between devices  61 us (27%)
  local copies, waits for them, and re-layouts  34.6 us (15%)
  other arithmetic  20.1 us (9%)
  matrix products  17.5 us (8%)
  starting transfers between devices  8.34 us (4%)
    all_to_all x1, blocking collectives, local_step(): received = lax.all_to_all(send_buf, 'ep', 1, 1, tiled=True)  71.4 us
    all_to_all x1, waiting for transfers between devices, local_step(): returned = lax.all_to_all(returned, 'ep', 1, 1, tiled=True)  61 us
    dot_general x1, matrix products, local_step(): jnp.einsum('abecf,efd->abecd', inner_act, w_down, preferred_element_type=...  12.3 us
    gather x1, local copies, waits for them, and re-layouts, local_step(): jnp.take(returned.reshape(n_slots, d_model), slot_ids, axis=0)  11.6 us
    gather x1, local copies, waits for them, and re-layouts, local_step(): send_buf = jnp.take(tokens, source_row, axis=0, mode='fill', fill_value=0)  9.94 us
    all_to_all x1, blocking collectives, local_step(): returned = lax.all_to_all(expert_out, 'ep2', 0, 0, tiled=True)  8.47 us
    all_to_all x1, starting transfers between devices, local_step(): returned = lax.all_to_all(returned, 'ep', 1, 1, tiled=True)  8.34 us
    scatter-add x1, other arithmetic, local_step(): jax.ops.segment_sum(token_of - tok_rows, slot_ids, num_segments=n_slots)  7.62 us
  transfers between devices with their start and end apart: 1, of which 1 were waited for; matrix products, arithmetic and copies ran while one was open for 0% of the time, Pallas kernels for 0%

commit v1 on v0

v1 whole, which is shorter than its diff:
```python
import functools

import jax
import jax.numpy as jnp
from jax import lax
from jax.experimental import pallas as pl
from jax.experimental.pallas import tpu as pltpu
from jax.sharding import PartitionSpec as P

MESH = pl.DeviceIdType.MESH
STEP = 37
BACK = 45


def pick(arr, i):
    return arr[:, i:i + 1]


def kernel(idx_ref, gates_ref, tok_ref, wg_hbm, wu_hbm, wd_hbm, out_ref,
           wg, wu, wd, sbuf, rbuf, ybuf, ret, rm_ref, gk_ref, acc, hbuf,
           wsem, ssem, rsem, s2sem, r2sem):
    c = lax.axis_index('ep2')
    e = lax.axis_index('ep')
    mx = e % 4
    my = (e // 4) % 4
    mz = e // 16
    bf = jnp.bfloat16
    f32 = jnp.float32

    cps = [pltpu.make_async_copy(wg_hbm, wg, wsem.at[0]), pltpu.make_async_copy(wu_hbm, wu, wsem.at[1]),
           pltpu.make_async_copy(wd_hbm, wd, wsem.at[2])]
    for q in cps:
        q.start()

    def target(i, sign):
        k = (i * STEP) % 128
        dx = k % 4
        dy = (k // 4) % 4
        dz = (k // 16) % 4
        dc = k // 64
        x = (mx + sign * dx + 4) % 4
        y = (my + sign * dy + 4) % 4
        z = (mz + sign * dz + 4) % 4
        return (0, (c + dc) % 2, z * 16 + y * 4 + x)

    bar = pltpu.get_barrier_semaphore()

    def sig(i, carry):
        pl.semaphore_signal(bar, inc=1, device_id=target(i, 1), device_id_type=MESH)
        return carry

    lax.fori_loop(1, 128, sig, 0)

    idx = idx_ref[...]
    rel = ((idx - mx) & 3) + (((idx >> 2) - my) & 3) * 4 + (((idx >> 4) - mz) & 3) * 16 + (((idx >> 6) - c) & 1) * 64
    pos = (rel * BACK) & 127
    lane = lax.broadcasted_iota(jnp.int32, (128, 128), 1)
    row = lax.broadcasted_iota(jnp.int32, (128, 128), 0)
    m = jnp.zeros((128, 128), f32)
    gk = jnp.zeros((128, 128), f32)
    for j in range(8):
        hit = pick(pos, j) == lane
        m = jnp.where(hit, 1.0, m)
        gk = jnp.where(hit, gates_ref[:, j:j + 1], gk)
    lower = jnp.where(lane < row, 1.0, 0.0).astype(bf)
    rank = jnp.dot(lower, m.astype(bf), preferred_element_type=f32)
    rm_ref[...] = jnp.where(m > 0.5, rank + 1.0, 0.0).astype(bf)
    hi = gk.astype(bf)
    r1 = gk - hi.astype(f32)
    mid = r1.astype(bf)
    lo = (r1 - mid.astype(f32)).astype(bf)
    gk_ref[0:128, :] = hi
    gk_ref[128:256, :] = mid
    gk_ref[256:384, :] = lo

    def spread(b, n):
        k = lax.broadcasted_iota(jnp.int32, (128, n), 0)
        s = lax.broadcasted_iota(jnp.int32, (128, n), 1)
        return jnp.where(k == b * (n // 8) + (s >> 3), 1.0, 0.0).astype(bf)

    def build(b, carry):
        ex = spread(b, 128)
        slot = lax.broadcasted_iota(jnp.int32, (128, 128), 1)
        r = jnp.dot(rm_ref[...], ex, preferred_element_type=f32)
        dt = jnp.where(r == ((slot & 7) + 1).astype(f32), 1.0, 0.0)
        d = jnp.swapaxes(dt, 0, 1).astype(bf)
        for t in range(4):
            rows = jnp.dot(d, tok_ref[:, t * 512:(t + 1) * 512], preferred_element_type=f32).astype(bf)
            sbuf[pl.ds(b * 16, 16), :, t * 512:(t + 1) * 512] = rows.reshape(16, 8, 512)
        return carry

    lax.fori_loop(0, 8, build, 0)
    rbuf[0] = sbuf[0]
    pl.semaphore_wait(bar, 127)

    def out_copy(i):
        return pltpu.make_async_remote_copy(sbuf.at[i], rbuf.at[i], ssem.at[i], rsem.at[i], device_id=target(i, 1), device_id_type=MESH)

    def back_copy(i):
        return pltpu.make_async_remote_copy(ybuf.at[i], ret.at[i], s2sem.at[i], r2sem.at[i], device_id=target(i, -1), device_id_type=MESH)

    def loop(lo_, hi_, fn):
        def body(i, carry):
            fn(i)
            return carry
        lax.fori_loop(lo_, hi_, body, 0)

    loop(1, 128, lambda i: out_copy(i).start())
    for q in cps:
        q.wait()

    for g in range(4):
        lo_i, hi_i = max(1, g * 32), g * 32 + 32
        loop(lo_i, hi_i, lambda i: out_copy(i).wait_recv())

        def up(f, carry):
            fs = pl.ds(pl.multiple_of(f * 256, 256), 256)
            x = rbuf[g * 32:(g + 1) * 32].reshape(256, 2048)
            a = jnp.dot(x, wg[:, fs], preferred_element_type=f32)
            b = jnp.dot(x, wu[:, fs], preferred_element_type=f32)
            hbuf[:, fs] = (a * jax.nn.sigmoid(a) * b).astype(bf)
            return carry

        lax.fori_loop(0, 3, up, 0)

        def down(n, carry):
            ns = pl.ds(pl.multiple_of(n * 512, 512), 512)
            y = jnp.dot(hbuf[...], wd[:, ns], preferred_element_type=f32).astype(bf)
            ybuf[g * 32:(g + 1) * 32, :, ns] = y.reshape(32, 8, 512)
            return carry

        lax.fori_loop(0, 4, down, 0)
        if g == 0:
            ret[0] = ybuf[0]
        loop(lo_i, hi_i, lambda i: back_copy(i).start())

    for g in range(4):
        lo_i, hi_i = max(1, g * 32), g * 32 + 32
        ex = spread(g, 256)
        slot = lax.broadcasted_iota(jnp.int32, (128, 256), 1)
        r = jnp.dot(rm_ref[...], ex, preferred_element_type=f32)
        on = jnp.where(r == ((slot & 7) + 1).astype(f32), 1.0, 0.0)
        gx = jnp.dot(gk_ref[...], ex, preferred_element_type=f32)
        gx = (gx * jnp.concatenate([on, on, on], axis=0)).astype(bf)
        loop(lo_i, hi_i, lambda i: back_copy(i).wait_recv())

        def mix(n, carry):
            ns = pl.ds(pl.multiple_of(n * 256, 256), 256)
            y = ret[g * 32:(g + 1) * 32, :, ns].reshape(256, 256)
            p = jnp.dot(gx, y, preferred_element_type=f32)
            p = p[0:128] + p[128:256] + p[256:384]
            base = tok_ref[:, ns].astype(f32) if g == 0 else acc[:, ns]
            if g == 3:
                out_ref[:, ns] = (base + p).astype(bf)
            else:
                acc[:, ns] = base + p
            return carry

        lax.fori_loop(0, 8, mix, 0)

    loop(1, 128, lambda i: out_copy(i).wait_send())
    loop(1, 128, lambda i: back_copy(i).wait_send())


def solution(mesh):
    row_spec = P(('dp', 'ep2', 'ep'), None)
    weight_spec = P(('ep2', 'ep'), None, None)

    def local_step(tokens, expert_idx, gates, w_gate, w_up, w_down):
        vm = pl.BlockSpec(memory_space=pltpu.VMEM)
        anyw = pl.BlockSpec(memory_space=pl.ANY)
        bf = jnp.bfloat16
        return pl.pallas_call(
            kernel,
            out_shape=jax.ShapeDtypeStruct((128, 2048), bf),
            in_specs=[vm, vm, vm, anyw, anyw, anyw],
            out_specs=vm,
            scratch_shapes=[
                pltpu.VMEM((2048, 768), bf), pltpu.VMEM((2048, 768), bf), pltpu.VMEM((768, 2048), bf),
                pltpu.VMEM((128, 8, 2048), bf), pltpu.VMEM((128, 8, 2048), bf),
                pltpu.VMEM((128, 8, 2048), bf), pltpu.VMEM((128, 8, 2048), bf),
                pltpu.VMEM((128, 128), bf), pltpu.VMEM((384, 128), bf),
                pltpu.VMEM((128, 2048), jnp.float32), pltpu.VMEM((256, 768), bf),
                pltpu.SemaphoreType.DMA((3,)),
                pltpu.SemaphoreType.DMA((128,)), pltpu.SemaphoreType.DMA((128,)),
                pltpu.SemaphoreType.DMA((128,)), pltpu.SemaphoreType.DMA((128,)),
            ],
            compiler_params=pltpu.CompilerParams(collective_id=0, has_side_effects=True, vmem_limit_bytes=60 * 1024 * 1024),
        )(expert_idx, gates, tokens, w_gate[0], w_up[0], w_down[0])

    return jax.shard_map(local_step, mesh=mesh, in_specs=(row_spec, row_spec, row_spec, weight_spec, weight_spec, weight_spec),
                         out_specs=row_spec, check_vma=False)
```

time: 229 us -> 149 us (0.65)
  the two profiles are of different devices: /device:TPU:1 before, /device:TPU:43 now
where the time goes in v1:
time: 149 us
  Pallas kernels  144 us (97%)
  local copies, waits for them, and re-layouts  4.7 us (3%)
    pallas_call x1, Pallas kernels, local_step(): pl.pallas_call(kernel, out_shape=jax.ShapeDtypeStruct((128, 2048), bf), i...  144 us
    unnamed x3, local copies, waits for them, and re-layouts  4.7 us

profile of v1, /device:TPU:43, one launch (start us, length us, event | category | flops | bytes accessed | tf_op | source)
XLA Modules:
  0.0 149.2 jit_solution(11200237509352192712)
XLA Ops:
  0.0 1.4 copy.7.idx_ref
  1.4 1.4 copy.8.gates_ref
  2.8 144.5 %shard_map.64 = bf16[128,2048]{1,0:T(8,128)(2,1)} custom-call(s32[128,8]{1,0:T(8,128)} %copy.7.idx_ref, f32[128,8]{1,0:T(8,128)} %copy.8.gates_ref, bf16[128,2048]{1,0:T(8,128)(2,1)} %tok_ref.1, bf16[2048,768]{1,0:T(8,128)(2,1)} %bitcast.3, bf16[2048,768]{1,0:T(8,128)(2,1)} %bitcast.4, bf16[768,2048]{1,0:T(8,128)(2,1)} %bitcast.5), custom_call_target="tpu_custom_call" | custom-call | tf_op jit(solution)/shard_map/pallas_call | solution.py:173
  147.3 1.9 %copy.10 = bf16[128,2048]{1,0:T(8,128)(2,1)} copy(bf16[128,2048]{1,0:T(8,128)(2,1)} %shard_map.64) | data formatting | bytes 1048576

commit v2 on v0

v2 whole, which is shorter than its diff:
```python
import functools

import jax
import jax.numpy as jnp
from jax import lax
from jax.experimental import pallas as pl
from jax.experimental.pallas import tpu as pltpu
from jax.sharding import PartitionSpec as P

MESH = pl.DeviceIdType.MESH
CUT = 10


def dec(j):
    return j % 3 + 1, (j % 9) // 3 + 1, j // 9


def third(q, u, v):
    return (q - u - v + 8) % 3 + 1


def slot_codes():
    codes = [0] * 128
    for j in range(18):
        u, v, dc = dec(j)
        for q in range(3):
            off = [0, 0, 0]
            off[q], off[(q + 1) % 3], off[(q + 2) % 3] = u, v, third(q, u, v)
            codes[3 * j + q] = off[0] + 4 * off[1] + 16 * off[2] + 64 * dc
            off = [0, 0, 0]
            off[(q + 1) % 3], off[(q + 2) % 3] = u, v
            codes[54 + 3 * j + q] = off[0] + 4 * off[1] + 16 * off[2] + 64 * dc
    for k in range(6):
        for m in range(3):
            codes[108 + 3 * k + m] = (k % 3 + 1) * 4 ** m + 64 * (k // 3)
    codes[126] = 64
    assert sorted(codes) == list(range(128))
    return codes


def loop(lo, hi, fn):
    def body(i, carry):
        fn(i)
        return carry
    lax.fori_loop(lo, hi, body, 0)


def each(*fns):
    def body(j):
        for q in range(3):
            for fn in fns:
                fn(j, q)
    return body


class Exchange:
    def __init__(self, co, core, sign, src, dst, rel, ssem, fsem, asem, rsem):
        self.co, self.core, self.sign = co, core, sign
        self.src, self.dst, self.rel = src, dst, rel
        self.ssem, self.fsem, self.asem, self.rsem = ssem, fsem, asem, rsem

    def to(self, axis, off, dc):
        p = list(self.co)
        if axis is not None:
            p[axis] = (p[axis] + self.sign * off + 4) % 4
        return (0, (self.core + dc) % 2, p[2] * 16 + p[1] * 4 + p[0])

    def copy(self, a, b, s, r, target):
        return pltpu.make_async_remote_copy(a, b, s, r, device_id=target, device_id_type=MESH)

    def a1(self, j, q):
        u, v, dc = dec(j)
        s = 3 * j + q
        self.copy(self.src.at[s], self.rel.at[s], self.ssem, self.asem.at[j], self.to(q, u, 0)).start()

    def a2(self, j, q):
        u, v, dc = dec(j)
        s = 3 * j + q
        self.copy(self.rel.at[s], self.rel.at[54 + s], self.fsem, self.asem.at[18 + j], self.to((q + 1) % 3, v, 0)).start()

    def a3(self, j, q):
        u, v, dc = dec(j)
        s = 3 * j + q
        self.copy(self.rel.at[54 + s], self.dst.at[s], self.fsem, self.rsem.at[j // CUT], self.to((q + 2) % 3, third(q, u, v), dc)).start()

    def b1(self, j, q):
        u, v, dc = dec(j)
        s = 3 * j + q
        self.copy(self.src.at[54 + s], self.rel.at[108 + s], self.ssem, self.asem.at[36 + j], self.to((q + 1) % 3, u, 0)).start()

    def b2(self, j, q):
        u, v, dc = dec(j)
        s = 3 * j + q
        self.copy(self.rel.at[108 + s], self.dst.at[54 + s], self.fsem, self.rsem.at[2 + j // CUT], self.to((q + 2) % 3, v, dc)).start()

    def c1(self, k, q):
        s = 108 + 3 * k + q
        self.copy(self.src.at[s], self.dst.at[s], self.ssem, self.rsem.at[4], self.to(q, k % 3 + 1, k // 3)).start()

    def c0(self):
        self.copy(self.src.at[126], self.dst.at[126], self.ssem, self.rsem.at[4], self.to(None, 0, 1)).start()

    def wait(self, ref, sem):
        pltpu.make_async_remote_copy(ref, ref, self.ssem, sem, device_id=self.to(None, 0, 1), device_id_type=MESH).wait_recv()

    def wait_a1(self, j):
        self.wait(self.rel.at[pl.ds(3 * j, 3)], self.asem.at[j])

    def wait_a2(self, j):
        self.wait(self.rel.at[pl.ds(54 + 3 * j, 3)], self.asem.at[18 + j])

    def wait_b1(self, j):
        self.wait(self.rel.at[pl.ds(108 + 3 * j, 3)], self.asem.at[36 + j])

    def wait_group(self, g):
        lo, n = GROUPS[g]
        n = n - 1 if g == 4 else n
        self.wait(self.dst.at[pl.ds(lo, n)], self.rsem.at[g])

    def drain(self):
        self.wait(self.src.at[pl.ds(0, 127)], self.ssem)
        self.wait(self.rel, self.fsem)


GROUPS = ((0, 3 * CUT), (3 * CUT, 54 - 3 * CUT), (54, 3 * CUT), (54 + 3 * CUT, 54 - 3 * CUT), (108, 20))


def kernel(code_ref, idx_ref, gates_ref, tok_ref, wg_hbm, wu_hbm, wd_hbm, out_ref,
           wg, wu, wd, sbuf, rbuf, ybuf, ret, rel1, rel2, rm_ref, gk_ref, acc, hbuf,
           wsem, ssem, asem1, rsem1, asem2, rsem2):
    c = lax.axis_index('ep2')
    e = lax.axis_index('ep')
    mx, my, mz = e % 4, (e // 4) % 4, e // 16
    bf = jnp.bfloat16
    f32 = jnp.float32

    cps = [pltpu.make_async_copy(wg_hbm, wg, wsem.at[0]), pltpu.make_async_copy(wu_hbm, wu, wsem.at[1]),
           pltpu.make_async_copy(wd_hbm, wd, wsem.at[2])]
    for q in cps:
        q.start()
    go = Exchange((mx, my, mz), c, 1, sbuf, rbuf, rel1, ssem.at[0], ssem.at[1], asem1, rsem1)
    back = Exchange((mx, my, mz), c, -1, ybuf, ret, rel2, ssem.at[2], ssem.at[3], asem2, rsem2)

    bar = pltpu.get_barrier_semaphore()

    def sig(k):
        for axis in range(3):
            for dc in range(2):
                pl.semaphore_signal(bar, inc=1, device_id=go.to(axis, k, dc), device_id_type=MESH)

    loop(1, 4, sig)
    pl.semaphore_signal(bar, inc=1, device_id=go.to(None, 0, 1), device_id_type=MESH)

    idx = idx_ref[...]
    code = ((idx - mx) & 3) + (((idx >> 2) - my) & 3) * 4 + (((idx >> 4) - mz) & 3) * 16 + (((idx >> 6) - c) & 1) * 64
    want = code_ref[0:1, :]
    lane = lax.broadcasted_iota(jnp.int32, (128, 128), 1)
    row = lax.broadcasted_iota(jnp.int32, (128, 128), 0)
    m = jnp.zeros((128, 128), f32)
    gk = jnp.zeros((128, 128), f32)
    for j in range(8):
        hit = code[:, j:j + 1] == want
        m = jnp.where(hit, 1.0, m)
        gk = jnp.where(hit, gates_ref[:, j:j + 1], gk)
    lower = jnp.where(lane < row, 1.0, 0.0).astype(bf)
    rank = jnp.dot(lower, m.astype(bf), preferred_element_type=f32)
    rm_ref[...] = jnp.where(m > 0.5, rank + 1.0, 0.0).astype(bf)
    hi = gk.astype(bf)
    r1 = gk - hi.astype(f32)
    mid = r1.astype(bf)
    lo = (r1 - mid.astype(f32)).astype(bf)
    gk_ref[0:128, :] = hi
    gk_ref[128:256, :] = mid
    gk_ref[256:384, :] = lo

    def spread(first, n):
        k = lax.broadcasted_iota(jnp.int32, (128, n), 0)
        s = lax.broadcasted_iota(jnp.int32, (128, n), 1)
        return jnp.where(k == first + (s >> 3), 1.0, 0.0).astype(bf)

    def chosen(first, n, ex):
        slot = lax.broadcasted_iota(jnp.int32, (128, n), 1)
        r = jnp.dot(rm_ref[...], ex, preferred_element_type=f32)
        return jnp.where(r == ((slot & 7) + 1).astype(f32), 1.0, 0.0)

    def build(b):
        d = jnp.swapaxes(chosen(b * 16, 128, spread(b * 16, 128)), 0, 1).astype(bf)
        for t in range(4):
            rows = jnp.dot(d, tok_ref[:, t * 512:(t + 1) * 512], preferred_element_type=f32).astype(bf)
            sbuf[pl.ds(b * 16, 16), :, t * 512:(t + 1) * 512] = rows.reshape(16, 8, 512)

    loop(0, 8, build)
    rbuf[127] = sbuf[127]
    pl.semaphore_wait(bar, 19)

    def ffn(g):
        lo_s, n = GROUPS[g]
        rows = n * 8

        def up(f):
            fs = pl.ds(pl.multiple_of(f * 256, 256), 256)
            x = rbuf[lo_s:lo_s + n].reshape(rows, 2048)
            a = jnp.dot(x, wg[:, fs], preferred_element_type=f32)
            b = jnp.dot(x, wu[:, fs], preferred_element_type=f32)
            hbuf[0:rows, fs] = (a * jax.nn.sigmoid(a) * b).astype(bf)

        loop(0, 3, up)

        def down(t):
            ns = pl.ds(pl.multiple_of(t * 512, 512), 512)
            y = jnp.dot(hbuf[0:rows, :], wd[:, ns], preferred_element_type=f32).astype(bf)
            ybuf[lo_s:lo_s + n, :, ns] = y.reshape(n, 8, 512)

        loop(0, 4, down)

    def mix(g, first, last):
        lo_s, n = GROUPS[g]
        rows = n * 8
        ex = spread(lo_s, rows)
        on = chosen(lo_s, rows, ex)
        gx = jnp.dot(gk_ref[...], ex, preferred_element_type=f32)
        gx = (gx * jnp.concatenate([on, on, on], axis=0)).astype(bf)
        back.wait_group(g)

        def part(t):
            ns = pl.ds(pl.multiple_of(t * 256, 256), 256)
            y = ret[lo_s:lo_s + n, :, ns].reshape(rows, 256)
            p = jnp.dot(gx, y, preferred_element_type=f32)
            p = p[0:128] + p[128:256] + p[256:384]
            base = tok_ref[:, ns].astype(f32) if first else acc[:, ns]
            if last:
                out_ref[:, ns] = (base + p).astype(bf)
            else:
                acc[:, ns] = base + p

        loop(0, 8, part)

    def fwd(x, wait, move):
        def body(j):
            wait(j)
            for q in range(3):
                move(j, q)
        return body

    loop(0, 18, each(go.a1))

    def second(j):
        go.wait_a1(j)
        for q in range(3):
            go.a2(j, q)
            go.b1(j, q)

    loop(0, 18, second)
    go.c0()
    loop(0, 6, each(go.c1))

    def third_hop(j):
        go.wait_a2(j)
        for q in range(3):
            go.a3(j, q)
        go.wait_b1(j)
        for q in range(3):
            go.b2(j, q)

    loop(0, 18, third_hop)
    for q in cps:
        q.wait()

    go.wait_group(0)
    ffn(0)
    loop(0, CUT, each(back.a1))
    go.wait_group(1)
    ffn(1)
    loop(CUT, 18, each(back.a1))
    loop(0, CUT, fwd(back, back.wait_a1, back.a2))
    go.wait_group(2)
    ffn(2)
    loop(0, CUT, each(back.b1))
    loop(CUT, 18, fwd(back, back.wait_a1, back.a2))
    go.wait_group(3)
    ffn(3)
    loop(CUT, 18, each(back.b1))
    loop(0, CUT, fwd(back, back.wait_a2, back.a3))
    go.wait_group(4)
    ffn(4)
    ret[127] = ybuf[127]
    back.c0()
    loop(0, 6, each(back.c1))
    loop(CUT, 18, fwd(back, back.wait_a2, back.a3))
    loop(0, 18, fwd(back, back.wait_b1, back.b2))
    go.drain()
    mix(0, True, False)
    mix(1, False, False)
    mix(4, False, False)
    mix(2, False, False)
    mix(3, False, True)
    back.drain()


def solution(mesh):
    row_spec = P(('dp', 'ep2', 'ep'), None)
    weight_spec = P(('ep2', 'ep'), None, None)

    def local_step(tokens, expert_idx, gates, w_gate, w_up, w_down):
        vm = pl.BlockSpec(memory_space=pltpu.VMEM)
        anyw = pl.BlockSpec(memory_space=pl.ANY)
        bf = jnp.bfloat16
        codes = jnp.broadcast_to(jnp.array(slot_codes(), jnp.int32)[None, :], (8, 128))
        dma = pltpu.SemaphoreType.DMA
        return pl.pallas_call(
            kernel,
            out_shape=jax.ShapeDtypeStruct((128, 2048), bf),
            in_specs=[vm, vm, vm, vm, anyw, anyw, anyw],
            out_specs=vm,
            scratch_shapes=[
                pltpu.VMEM((2048, 768), bf), pltpu.VMEM((2048, 768), bf), pltpu.VMEM((768, 2048), bf),
                pltpu.VMEM((128, 8, 2048), bf), pltpu.VMEM((128, 8, 2048), bf),
                pltpu.VMEM((128, 8, 2048), bf), pltpu.VMEM((128, 8, 2048), bf),
                pltpu.VMEM((162, 8, 2048), bf), pltpu.VMEM((162, 8, 2048), bf),
                pltpu.VMEM((128, 128), bf), pltpu.VMEM((384, 128), bf),
                pltpu.VMEM((128, 2048), jnp.float32), pltpu.VMEM((256, 768), bf),
                dma((3,)), dma((4,)), dma((54,)), dma((5,)), dma((54,)), dma((5,)),
            ],
            compiler_params=pltpu.CompilerParams(collective_id=0, has_side_effects=True, vmem_limit_bytes=60 * 1024 * 1024),
        )(codes, expert_idx, gates, tokens, w_gate[0], w_up[0], w_down[0])

    return jax.shard_map(local_step, mesh=mesh, in_specs=(row_spec, row_spec, row_spec, weight_spec, weight_spec, weight_spec),
                         out_specs=row_spec, check_vma=False)
```

time: 229 us -> 114 us (0.50)
  Pallas kernels: 0 us -> 108 us
  blocking collectives: 86.9 us -> 0 us
  waiting for transfers between devices: 61 us -> 0 us
  local copies, waits for them, and re-layouts: 34.6 us -> 5.95 us
  other arithmetic: 20.1 us -> 0 us
  matrix products: 17.5 us -> 0 us
  starting transfers between devices: 8.34 us -> 0 us
    pallas_call x0 -> x1, Pallas kernels: none -> 108 us  [local_step(): pl.pallas_call(kernel, out_shape=jax.ShapeDtypeStruct((128, 2048), bf), i...]
    all_to_all x3 -> x0, blocking collectives: 86.9 us -> none  [the longest x1 71.4 us: local_step(): received = lax.all_to_all(send_buf, 'ep', 1, 1, tiled=True)]
    all_to_all x1 -> x0, waiting for transfers between devices: 61 us -> none  [local_step(): returned = lax.all_to_all(returned, 'ep', 1, 1, tiled=True)]
    gather x2 -> x0, local copies, waits for them, and re-layouts: 21.5 us -> none  [the longest x1 11.6 us: local_step(): jnp.take(returned.reshape(n_slots, d_model), slot_ids, axis=0)]
    dot_general x2 -> x0, matrix products: 17.5 us -> none  [the longest x1 12.3 us: local_step(): jnp.einsum('abecf,efd->abecd', inner_act, w_down, preferred_element_type=...]
    all_to_all x1 -> x0, starting transfers between devices: 8.34 us -> none  [local_step(): returned = lax.all_to_all(returned, 'ep', 1, 1, tiled=True)]
    scatter-add x1 -> x0, other arithmetic: 7.62 us -> none  [local_step(): jax.ops.segment_sum(token_of - tok_rows, slot_ids, num_segments=n_slots)]
    all_to_all x3 -> x0, local copies, waits for them, and re-layouts: 7.6 us -> none  [the longest x1 4.74 us: local_step(): returned = lax.all_to_all(returned, 'ep', 1, 1, tiled=True)]
  transfers between devices with their start and end apart: 1 -> 0, of which waited for: 1 -> 0; matrix products, arithmetic and copies ran while one was open for 0% -> 0% of each run, Pallas kernels for 0% -> 0%
where the time goes in v2:
time: 114 us
  Pallas kernels  108 us (95%)
  local copies, waits for them, and re-layouts  5.95 us (5%)
    pallas_call x1, Pallas kernels, local_step(): pl.pallas_call(kernel, out_shape=jax.ShapeDtypeStruct((128, 2048), bf), i...  108 us
    unnamed x3, local copies, waits for them, and re-layouts  4.7 us

profile of v2, /device:TPU:1, one launch (start us, length us, event | category | flops | bytes accessed | tf_op | source)
XLA Modules:
  0.0 113.8 jit_solution(49946719028097259)
XLA Ops:
  0.0 1.4 %copy.8.idx_ref = s32[128,8]{1,0:T(8,128)} copy(s32[128,8]{0,1:T(8,128)} %param.8) | data formatting | bytes 8192 | tf_op args[1]
  1.4 1.4 %copy.9.gates_ref = f32[128,8]{1,0:T(8,128)} copy(f32[128,8]{0,1:T(8,128)} %param.9) | data formatting | bytes 8192 | tf_op args[2]
  2.8 1.2 %broadcast_in_dim.2.code_ref = s32[8,128]{1,0:T(8,128)} broadcast(s32[128]{0:T(128)} %constant.2.clone), dimensions={1} | broadcast | bytes 4608 | tf_op jit(solution)/shard_map/broadcast_in_dim | solution.py:308
  4.1 107.8 %shard_map.73 = bf16[128,2048]{1,0:T(8,128)(2,1)} custom-call(s32[8,128]{1,0:T(8,128)} %broadcast_in_dim.2.code_ref, s32[128,8]{1,0:T(8,128)} %copy.8.idx_ref, f32[128,8]{1,0:T(8,128)} %copy.9.gates_ref, bf16[128,2048]{1,0:T(8,128)(2,1)} %tok_ref.1, bf16[2048,768]{1,0:T(8,128)(2,1)} %bitcast.3, bf16[2048,768]{1,0:T(8,128)(2,1)} %bitcast.4, ...), custom_call_target="tpu_custom_call" | custom-call | tf_op jit(solution)/shard_map/pallas_call | solution.py:310
  111.9 1.9 %copy.11 = bf16[128,2048]{1,0:T(8,128)(2,1)} copy(bf16[128,2048]{1,0:T(8,128)(2,1)} %shard_map.73) | data formatting | bytes 1048576

commit v3 on v2

v3 whole, which is shorter than its diff:
```python
import jax
import jax.numpy as jnp
import numpy as np
from jax import lax
from jax.experimental import pallas as pl
from jax.experimental.pallas import tpu as pltpu
from jax.sharding import PartitionSpec as P

MESH = pl.DeviceIdType.MESH
CUT = 8
D = 2048
TURNS = 18
T = 128
HALF = (2, 4, 4, 4)
AXES = range(3)
NEXT = (1, 3, 2)
COLS = ((0, 768), (768, 640), (1408, 640))
WEIGHT = (1, 4, 16)


def dec(j):
    return j % 3 + 1, (j % 9) // 3 + 1, j // 9


def third(q, u, v):
    return (q - u - v + 8) % 3 + 1


def offsets(kind, j, q):
    off = [0, 0, 0]
    if kind == 0:
        u, v, dc = dec(j)
        off[q], off[(q + 1) % 3], off[(q + 2) % 3] = u, v, third(q, u, v)
    elif kind == 1:
        u, v, dc = dec(j)
        off[(q + 1) % 3], off[(q + 2) % 3] = u, v
    else:
        off[q], dc = j % 3 + 1, j // 3
    return off, dc


def slot_codes():
    codes = [0] * 128
    for kind, n in ((0, TURNS), (1, TURNS), (2, 6)):
        for j in range(n):
            for q in AXES:
                off, dc = offsets(kind, j, q)
                codes[54 * kind + 3 * j + q] = off[0] + 4 * off[1] + 16 * off[2] + 64 * dc
    codes[126] = 64
    assert sorted(codes) == list(range(128))
    return codes


def loop(lo, hi, fn):
    def body(i, carry):
        fn(i)
        return carry
    lax.fori_loop(lo, hi, body, 0)


def each(*fns):
    def body(j):
        for q in AXES:
            for fn in fns:
                fn(j, q)
    return body


def target(co, core, axis, off, dc):
    p = list(co)
    if axis is not None:
        p[axis] = (p[axis] + off) % 4
    return (0, (core + dc) % 2, p[2] * 16 + p[1] * 4 + p[0])


def iota(dim, *shape):
    return lax.broadcasted_iota(jnp.int32, shape, dim)


def onehot(mask, dtype=jnp.bfloat16):
    return jnp.where(mask, 1.0, 0.0).astype(dtype)


class Exchange:
    def __init__(self, co, core, sign, src, dst, rel, ssem, fsem, asem, rsem):
        self.co, self.core, self.sign = co, core, sign
        self.src, self.dst, self.rel = src, dst, rel
        self.ssem, self.fsem, self.asem, self.rsem = ssem, fsem, asem, rsem

    def to(self, axis, off, dc):
        return target(self.co, self.core, axis, self.sign * off + 4, dc)

    def copy(self, a, b, s, r, dest):
        return pltpu.make_async_remote_copy(a, b, s, r, device_id=dest, device_id_type=MESH)

    def a1(self, j, q):
        u, v, dc = dec(j)
        s = 3 * j + q
        self.copy(self.src.at[s], self.rel.at[s], self.ssem, self.asem.at[j], self.to(q, u, 0)).start()

    def a2(self, j, q):
        u, v, dc = dec(j)
        s = 3 * j + q
        self.copy(self.rel.at[s], self.rel.at[54 + s], self.fsem, self.asem.at[TURNS + j], self.to((q + 1) % 3, v, 0)).start()

    def a3(self, j, q):
        u, v, dc = dec(j)
        s = 3 * j + q
        self.copy(self.rel.at[54 + s], self.dst.at[s], self.fsem, self.rsem.at[(j + 10 - CUT) // 10], self.to((q + 2) % 3, third(q, u, v), dc)).start()

    def b1(self, j, q):
        u, v, dc = dec(j)
        s = 3 * j + q
        self.copy(self.src.at[54 + s], self.rel.at[108 + s], self.ssem, self.asem.at[2 * TURNS + j], self.to((q + 1) % 3, u, 0)).start()

    def b2(self, j, q):
        u, v, dc = dec(j)
        s = 3 * j + q
        self.copy(self.rel.at[108 + s], self.dst.at[54 + s], self.fsem, self.rsem.at[2 + (j + 10 - CUT) // 10], self.to((q + 2) % 3, v, dc)).start()

    def c1(self, k, q):
        s = 108 + 3 * k + q
        self.copy(self.src.at[s], self.dst.at[s], self.ssem, self.rsem.at[4], self.to(q, k % 3 + 1, k // 3)).start()

    def c0(self):
        self.copy(self.src.at[126], self.dst.at[126], self.ssem, self.rsem.at[4], self.to(None, 0, 1)).start()

    def wait(self, ref, sem):
        pltpu.make_async_remote_copy(ref, ref, self.ssem, sem, device_id=self.to(None, 0, 1), device_id_type=MESH).wait_recv()

    def wait_a1(self, j):
        self.wait(self.rel.at[pl.ds(3 * j, 3)], self.asem.at[j])

    def wait_a2(self, j):
        self.wait(self.rel.at[pl.ds(54 + 3 * j, 3)], self.asem.at[TURNS + j])

    def wait_b1(self, j):
        self.wait(self.rel.at[pl.ds(108 + 3 * j, 3)], self.asem.at[2 * TURNS + j])

    def wait_group(self, g):
        lo, n = GROUPS[g]
        n = n - 1 if g == 4 else n
        self.wait(self.dst.at[pl.ds(lo, n)], self.rsem.at[g])

    def drain(self):
        self.wait(self.src.at[pl.ds(0, 127)], self.ssem)
        self.wait(self.rel, self.fsem)


EARLY, LATE = 3 * CUT, 54 - 3 * CUT
GROUPS = ((0, EARLY), (EARLY, LATE), (54, EARLY), (54 + EARLY, LATE), (108, 20))


def kernel(code_hbm, idx_hbm, gates_hbm, tok_hbm, wg_hbm, wu_hbm, wd_hbm, out_ref,
           code_ref, idx_ref, gates_ref, tok_ref, wg, wu, wd, toka, idxa, bld, mid, rbuf, xg, ybuf, ret, rel2, rm_ref, gk_ref, acc, hbuf,
           *rest):
    gx_refs = rest[:5]
    wsem, ssem, tsem, isem, bsem, csem, asem2, rsem2 = rest[5:]
    c = lax.axis_index('ep2')
    e = lax.axis_index('ep')
    me = (e % 4, (e // 4) % 4, e // 16)
    bf = jnp.bfloat16
    f32 = jnp.float32

    cps = [pltpu.make_async_copy(wg_hbm, wg, wsem.at[0]), pltpu.make_async_copy(wu_hbm, wu, wsem.at[1]),
           pltpu.make_async_copy(wd_hbm, wd, wsem.at[2])]
    small = [pltpu.make_async_copy(a, b, wsem.at[3 + i]) for i, (a, b) in enumerate(
        ((idx_hbm, idx_ref), (tok_hbm, tok_ref), (gates_hbm, gates_ref), (code_hbm, code_ref)))]
    back = Exchange(me, c, -1, ybuf, ret, rel2, ssem.at[4], ssem.at[5], asem2, rsem2)

    def to(axis, off, dc):
        return target(me, c, axis, off, dc)

    for q in small:
        q.start()
    bar = pltpu.get_barrier_semaphore()

    def sig(k):
        for axis in AXES:
            for dc in range(2):
                pl.semaphore_signal(bar, inc=1, device_id=to(axis, k, dc), device_id_type=MESH)

    loop(1, 4, sig)
    pl.semaphore_signal(bar, inc=1, device_id=to(None, 0, 1), device_id_type=MESH)
    before = onehot(iota(0, T, T) < iota(1, T, T))

    def ranked(idx8, want):
        m = jnp.zeros(want.shape, f32)
        for j in range(8):
            m = jnp.where(idx8[j:j + 1, :] == want, 1.0, m)
        rank = jnp.dot(m.astype(bf), before, preferred_element_type=f32)
        return jnp.where(m > 0.5, rank + 1.0, 0.0)

    def select(idx8, p):
        k = iota(0, 32, 128)
        b, d = (p + 1) % 3, (p + 2) % 3
        want = (((c + (k >> 4)) & 1) * 64 + me[p] * WEIGHT[p] + ((me[b] + (k >> 2)) & 3) * WEIGHT[b]
                + ((me[d] + k) & 3) * WEIGHT[d])
        rm = ranked(idx8, want).astype(bf)
        ex = onehot((iota(0, 256, 32) >> 3) == iota(1, 256, 32))
        r = jnp.dot(ex, rm, preferred_element_type=f32)
        return onehot(r == ((iota(0, 256, T) & 7) + 1).astype(f32))

    def cols(p):
        return pl.ds(COLS[p][0], COLS[p][1])

    def build(p, a):
        n = COLS[p][1]
        if a == 0:
            rows = jnp.dot(select(idx_ref[...], p), tok_ref[:, cols(p)], preferred_element_type=f32).astype(bf)
        else:
            rows = jnp.dot(select(idxa[p, a - 1], p), toka[a - 1, :, cols(p)], preferred_element_type=f32).astype(bf)
        rows = rows.reshape(2, 4, 4, 8, n)
        for dc in range(2):
            mid[dc, 0, a, :, :, cols(p)] = rows[dc, 0]
            for v in NEXT:
                bld[dc, v - 1, a, :, :, cols(p)] = rows[dc, v]

    def remote(a, b, s, r, dest):
        return pltpu.make_async_remote_copy(a, b, s, r, device_id=dest, device_id_type=MESH)

    def take(ref, sem):
        remote(ref, ref, ssem.at[0], sem, to(None, 0, 1)).wait_recv()

    def gather_tokens():
        for u in (1, 3, 2):
            for p in AXES:
                remote(idx_ref, idxa.at[p, u - 1], ssem.at[0], isem.at[p, u - 1], to(p, u, 0)).start()
                if u != 2:
                    remote(tok_ref.at[:, cols(p)], toka.at[u - 1, :, cols(p)], ssem.at[1], tsem.at[p, u - 1], to(p, u, 0)).start()

    def pass_on(p, a):
        lo_c, n = COLS[p]
        part = pl.ds(lo_c, 384) if a == 1 else pl.ds(lo_c + 384, n - 384)
        remote(toka.at[a - 1, :, part], toka.at[1, :, part], ssem.at[6], tsem.at[p, 1], to(p, a, 0)).start()

    def second(dc, a, p):
        for v in NEXT:
            remote(bld.at[dc, v - 1, a, :, :, cols(p)], mid.at[dc, v, a, :, :, cols(p)], ssem.at[2], bsem.at[dc, p, v - 1],
                   to((p + 1) % 3, v, 0)).start()

    def place(p, v, w, dc, ref):
        if p == 0:
            return ref.at[dc, w, v, :, :, cols(0)]
        if p == 1:
            return ref.at[dc, v, :, w, :, cols(1)]
        return ref.at[dc, :, w, v, :, cols(2)]

    def last(dc, v):
        for p in AXES:
            if v:
                take(mid.at[dc, v, :, :, :, cols(p)], bsem.at[dc, p, v - 1])
            for w in range(1 - dc, 4):
                remote(mid.at[dc, v, :, w, :, cols(p)], place(p, v, w, dc, rbuf), ssem.at[3 + 4 * dc], csem.at[dc, p],
                       to((p + 2) % 3, w, dc) if w else to(None, 0, 1)).start()
            if dc == 0:
                place(p, v, 0, 0, rbuf)[...] = mid[0, v, :, 0, :, cols(p)]

    for q in small:
        q.wait()
    for p in AXES:
        build(p, 0)
    pl.semaphore_wait(bar, 19)
    for q in cps:
        q.start()
    gather_tokens()
    for dc in range(2):
        for p in AXES:
            second(dc, 0, p)
    for a in (1, 3):
        for p in AXES:
            take(toka.at[a - 1, :, cols(p)], tsem.at[p, a - 1])
            pass_on(p, a)
    for a in NEXT:
        for p in AXES:
            take(idxa.at[p, a - 1], isem.at[p, a - 1])
            if a == 2:
                take(toka.at[a - 1, :, cols(p)], tsem.at[p, a - 1])
            build(p, a)
            second(0, a, p)
    last(0, 0)
    for a in (1, 3):
        for p in AXES:
            second(1, a, p)

    rel = (((idx_ref[...] >> 6) - c) & 1) << 6
    for d in AXES:
        rel += (((idx_ref[...] >> (2 * d)) - me[d]) & 3) << (2 * d)
    want = code_ref[...]
    rm_ref[...] = jnp.swapaxes(ranked(rel, want), 0, 1).astype(bf)
    gk = jnp.zeros((T, T), f32)
    for j in range(8):
        gk = jnp.where(rel[j:j + 1, :] == want, gates_ref[j:j + 1, :], gk)
    gk = jnp.swapaxes(gk, 0, 1)
    hi = gk.astype(bf)
    r1 = gk - hi.astype(f32)
    md = r1.astype(bf)
    lo = (r1 - md.astype(f32)).astype(bf)
    gk_ref[...] = jnp.concatenate([hi, md, lo], axis=0)

    def spread(first, n):
        return onehot(iota(0, T, n) == first + (iota(1, T, n) >> 3))

    def chosen(n, ex):
        r = jnp.dot(rm_ref[...], ex, preferred_element_type=f32)
        return onehot(r == ((iota(1, T, n) & 7) + 1).astype(f32), f32)

    for g in range(5):
        ex = spread(GROUPS[g][0], GROUPS[g][1] * 8)
        on = chosen(GROUPS[g][1] * 8, ex)
        gx = jnp.dot(gk_ref[...], ex, preferred_element_type=f32)
        gx_refs[g][...] = (gx * jnp.concatenate([on, on, on], axis=0)).astype(bf)


    for v in NEXT:
        last(0, v)
    for p in AXES:
        second(1, 2, p)
    for v in (0, *NEXT):
        last(1, v)
    for q in cps:
        q.wait()

    def fetch(kind, lo_j, hi_j):
        def body(j):
            for q in AXES:
                off, dc = offsets(kind, j, q)
                xg[3 * (j - lo_j) + q] = rbuf[dc, off[2], off[1], off[0]]
        loop(lo_j, hi_j, body)

    def arrived(dc):
        if dc == 0:
            take(rbuf.at[0, 1:4, :, :, :, cols(0)], csem.at[0, 0])
            take(rbuf.at[0, :, :, 1:4, :, cols(1)], csem.at[0, 1])
            take(rbuf.at[0, :, 1:4, :, :, cols(2)], csem.at[0, 2])
        else:
            for p in AXES:
                take(rbuf.at[1, :, :, :, :, cols(p)], csem.at[1, p])

    def ffn(g):
        lo_s, n = GROUPS[g]
        rows = n * 8

        def up(f):
            fs = pl.ds(pl.multiple_of(f * 256, 256), 256)
            x = xg[0:n].reshape(rows, 2048)
            a = jnp.dot(x, wg[:, fs], preferred_element_type=f32)
            b = jnp.dot(x, wu[:, fs], preferred_element_type=f32)
            hbuf[0:rows, fs] = (a * jax.nn.sigmoid(a) * b).astype(bf)

        loop(0, 3, up)

        def down(t):
            ns = pl.ds(pl.multiple_of(t * 512, 512), 512)
            y = jnp.dot(hbuf[0:rows, :], wd[:, ns], preferred_element_type=f32).astype(bf)
            ybuf[lo_s:lo_s + n, :, ns] = y.reshape(n, 8, 512)

        loop(0, 4, down)

    def mix(g, first, last):
        lo_s, n = GROUPS[g]
        rows = n * 8
        gx = gx_refs[g][...]
        back.wait_group(g)

        def part(t):
            ns = pl.ds(pl.multiple_of(t * 256, 256), 256)
            y = ret[lo_s:lo_s + n, :, ns].reshape(rows, 256)
            p = jnp.dot(gx, y, preferred_element_type=f32)
            p = p[:T] + p[T:2 * T] + p[2 * T:]
            base = tok_ref[:, ns].astype(f32) if first else acc[:, ns]
            if last:
                out_ref[:, ns] = (base + p).astype(bf)
            else:
                acc[:, ns] = base + p

        loop(0, 8, part)

    def fwd(x, wait, move):
        def body(j):
            wait(j)
            for q in AXES:
                move(j, q)
        return body

    arrived(0)
    fetch(0, 0, CUT)
    ffn(0)
    loop(0, CUT, each(back.a1))
    fetch(1, 0, CUT)
    ffn(2)
    loop(0, CUT, each(back.b1))
    arrived(1)
    fetch(0, CUT, TURNS)
    ffn(1)
    loop(CUT, TURNS, each(back.a1))
    loop(0, CUT, fwd(back, back.wait_a1, back.a2))
    fetch(1, CUT, TURNS)
    ffn(3)
    loop(CUT, TURNS, each(back.b1))
    loop(CUT, TURNS, fwd(back, back.wait_a1, back.a2))
    fetch(2, 0, 6)
    for dc in range(2):
        xg[19 - dc] = rbuf[dc, 0, 0, 0]
    ffn(4)
    ret[127] = ybuf[127]
    back.c0()
    loop(0, 6, each(back.c1))
    loop(0, CUT, fwd(back, back.wait_a2, back.a3))
    loop(0, CUT, fwd(back, back.wait_b1, back.b2))
    loop(CUT, TURNS, fwd(back, back.wait_a2, back.a3))
    loop(CUT, TURNS, fwd(back, back.wait_b1, back.b2))
    take(idxa, ssem.at[0])
    take(toka.at[0:2], ssem.at[1])
    take(toka.at[0], ssem.at[6])
    take(bld, ssem.at[2])
    take(mid.at[0, :, :, 1:4], ssem.at[3])
    take(mid.at[1], ssem.at[7])
    mix(4, True, False)
    mix(0, False, False)
    mix(2, False, False)
    mix(1, False, False)
    mix(3, False, True)
    back.drain()


def solution(mesh):
    row_spec = P(('dp', 'ep2', 'ep'), None)
    weight_spec = P(('ep2', 'ep'), None, None)

    def local_step(tokens, expert_idx, gates, w_gate, w_up, w_down):
        vm = pl.BlockSpec(memory_space=pltpu.VMEM)
        anyw = pl.BlockSpec(memory_space=pl.ANY)
        bf = jnp.bfloat16
        codes = jnp.array(np.repeat(np.array(slot_codes(), np.int32)[:, None], 128, axis=1))
        dma = pltpu.SemaphoreType.DMA

        def vmem(*shape):
            return pltpu.VMEM(shape, bf)

        def rows(*shape):
            return vmem(*shape, 8, D)

        return pl.pallas_call(
            kernel,
            out_shape=jax.ShapeDtypeStruct((128, D), bf),
            in_specs=[anyw] * 7,
            out_specs=vm,
            scratch_shapes=[
                pltpu.VMEM((T, T), jnp.int32), pltpu.VMEM((8, T), jnp.int32), pltpu.VMEM((8, T), jnp.float32), vmem(T, D),
                vmem(D, 768), vmem(D, 768), vmem(768, D),
                vmem(3, T, D), pltpu.VMEM((3, 3, 8, T), jnp.int32),
                rows(2, 3, 4, 4), rows(*HALF), rows(*HALF), rows(32), rows(T), rows(T), rows(9 * TURNS),
                vmem(T, T), vmem(3 * T, T), pltpu.VMEM((T, D), jnp.float32), vmem(256, 768),
                *[vmem(3 * T, n * 8) for _, n in GROUPS],
                *[dma(n) for n in ((7,), (8,), (3, 3), (3, 3), (2, 3, 3), (2, 3), (3 * TURNS,), (5,))],
            ],
            compiler_params=pltpu.CompilerParams(collective_id=0, has_side_effects=True, vmem_limit_bytes=60 << 20),
        )(codes, expert_idx.T, gates.T, tokens, w_gate[0], w_up[0], w_down[0])

    return jax.shard_map(local_step, mesh=mesh, in_specs=(row_spec, row_spec, row_spec, weight_spec, weight_spec, weight_spec),
                         out_specs=row_spec, check_vma=False)
```

time: 114 us -> 98.8 us (0.87)
  Pallas kernels: 108 us -> 96.7 us
  local copies, waits for them, and re-layouts: 5.95 us -> 1.88 us
    pallas_call x1, Pallas kernels: 108 us -> 96.7 us  [local_step(): pl.pallas_call(kernel, out_shape=jax.ShapeDtypeStruct((128, D), bf), in_s...]
    unnamed x3 -> x1, local copies, waits for them, and re-layouts: 4.7 us -> 1.88 us
    broadcast_in_dim x1 -> x0, local copies, waits for them, and re-layouts: 1.25 us -> none  [local_step(): jnp.broadcast_to(jnp.array(slot_codes(), jnp.int32)[None, :], (8, 128))]
where the time goes in v3:
time: 98.8 us; the launch traced here: 98.6 us
  Pallas kernels  96.7 us (98%)
  local copies, waits for them, and re-layouts  1.88 us (2%)
    pallas_call x1, Pallas kernels, local_step(): pl.pallas_call(kernel, out_shape=jax.ShapeDtypeStruct((128, D), bf), in_s...  96.7 us

profile of v3, /device:TPU:1, one launch (start us, length us, event | category | flops | bytes accessed | tf_op | source)
XLA Modules:
  0.0 98.6 jit_solution(12978505152413952541)
XLA Ops:
  0.0 96.7 %shard_map.73 = bf16[128,2048]{1,0:T(8,128)(2,1)} custom-call(s32[128,128]{1,0:T(8,128)} %constant.2.clone.code_hbm, s32[8,128]{1,0:T(8,128)} %bitcast.8, f32[8,128]{1,0:T(8,128)} %bitcast.9, bf16[128,2048]{1,0:T(8,128)(2,1)} %tok_hbm.1, bf16[2048,768]{1,0:T(8,128)(2,1)} %bitcast.5, bf16[2048,768]{1,0:T(8,128)(2,1)} %bitcast.6, bf16[768,2048]{1,0:T(8,128)(2,1)} %bitcast.7), custom_call_target="tpu_custom_call" | custom-call | tf_op jit(solution)/shard_map/pallas_call | solution.py:444
  96.7 1.9 %copy.9 = bf16[128,2048]{1,0:T(8,128)(2,1)} copy(bf16[128,2048]{1,0:T(8,128)(2,1)} %shard_map.73) | data formatting | bytes 1048576

commit v4 on v3

--- a/solution.py
+++ b/solution.py
@@ -264,9 +264,8 @@
     for q in cps:
         q.start()
     gather_tokens()
-    for dc in range(2):
-        for p in AXES:
-            second(dc, 0, p)
+    for p in AXES:
+        second(0, 0, p)
     for a in (1, 3):
         for p in AXES:
             take(toka.at[a - 1, :, cols(p)], tsem.at[p, a - 1])
@@ -279,7 +278,7 @@
             build(p, a)
             second(0, a, p)
     last(0, 0)
-    for a in (1, 3):
+    for a in (0, 1, 3):
         for p in AXES:
             second(1, a, p)
 
@@ -342,20 +341,20 @@
         rows = n * 8
 
         def up(f):
-            fs = pl.ds(pl.multiple_of(f * 256, 256), 256)
+            fs = pl.ds(pl.multiple_of(f * 768, 768), 768)
             x = xg[0:n].reshape(rows, 2048)
             a = jnp.dot(x, wg[:, fs], preferred_element_type=f32)
             b = jnp.dot(x, wu[:, fs], preferred_element_type=f32)
             hbuf[0:rows, fs] = (a * jax.nn.sigmoid(a) * b).astype(bf)
 
-        loop(0, 3, up)
+        loop(0, 1, up)
 
         def down(t):
-            ns = pl.ds(pl.multiple_of(t * 512, 512), 512)
+            ns = pl.ds(pl.multiple_of(t * 2048, 2048), 2048)
             y = jnp.dot(hbuf[0:rows, :], wd[:, ns], preferred_element_type=f32).astype(bf)
-            ybuf[lo_s:lo_s + n, :, ns] = y.reshape(n, 8, 512)
-
-        loop(0, 4, down)
+            ybuf[lo_s:lo_s + n, :, ns] = y.reshape(n, 8, 2048)
+
+        loop(0, 1, down)
 
     def mix(g, first, last):
         lo_s, n = GROUPS[g]
@@ -364,8 +363,8 @@
         back.wait_group(g)
 
         def part(t):
-            ns = pl.ds(pl.multiple_of(t * 256, 256), 256)
-            y = ret[lo_s:lo_s + n, :, ns].reshape(rows, 256)
+            ns = pl.ds(pl.multiple_of(t * 2048, 2048), 2048)
+            y = ret[lo_s:lo_s + n, :, ns].reshape(rows, 2048)
             p = jnp.dot(gx, y, preferred_element_type=f32)
             p = p[:T] + p[T:2 * T] + p[2 * T:]
             base = tok_ref[:, ns].astype(f32) if first else acc[:, ns]
@@ -374,7 +373,7 @@
             else:
                 acc[:, ns] = base + p
 
-        loop(0, 8, part)
+        loop(0, 1, part)
 
     def fwd(x, wait, move):
         def body(j):

time: 98.8 us -> 96.5 us (0.977); the launches traced: 98.6 us -> 95.1 us
  Pallas kernels: 96.7 us -> 93.2 us
    pallas_call x1, Pallas kernels: 96.7 us -> 93.2 us  [local_step(): pl.pallas_call(kernel, out_shape=jax.ShapeDtypeStruct((128, D), bf), in_s...]
where the time goes in v4:
time: 96.5 us; the launch traced here: 95.1 us
  Pallas kernels  93.2 us (97%)
  local copies, waits for them, and re-layouts  1.88 us (2%)
    pallas_call x1, Pallas kernels, local_step(): pl.pallas_call(kernel, out_shape=jax.ShapeDtypeStruct((128, D), bf), in_s...  93.2 us

profile of v4, /device:TPU:1, one launch (start us, length us, event | category | flops | bytes accessed | tf_op | source)
XLA Modules:
  0.0 95.1 jit_solution(9328982427898811922)
XLA Ops:
  0.0 93.2 %shard_map.73 = bf16[128,2048]{1,0:T(8,128)(2,1)} custom-call(s32[128,128]{1,0:T(8,128)} %constant.2.clone.code_hbm, s32[8,128]{1,0:T(8,128)} %bitcast.8, f32[8,128]{1,0:T(8,128)} %bitcast.9, bf16[128,2048]{1,0:T(8,128)(2,1)} %tok_hbm.1, bf16[2048,768]{1,0:T(8,128)(2,1)} %bitcast.5, bf16[2048,768]{1,0:T(8,128)(2,1)} %bitcast.6, bf16[768,2048]{1,0:T(8,128)(2,1)} %bitcast.7), custom_call_target="tpu_custom_call" | custom-call | tf_op jit(solution)/shard_map/pallas_call | solution.py:443
  93.2 1.9 %copy.9 = bf16[128,2048]{1,0:T(8,128)(2,1)} copy(bf16[128,2048]{1,0:T(8,128)(2,1)} %shard_map.73) | data formatting | bytes 1048576

commit v5 on v0

v5 whole, which is shorter than its diff:
```python
import jax
import jax.numpy as jnp
from jax import lax
from jax.experimental import pallas as pl
from jax.experimental.pallas import tpu as pltpu
from jax.sharding import PartitionSpec as P

MESH = pl.DeviceIdType.MESH
D = 2048
T = 128
F = 768
AXES = range(3)
CORES = range(2)
NEXT = (1, 3, 2)
COLS = ((0, 768), (768, 640), (1408, 640))
SPLIT = 384
WEIGHT = (1, 4, 16)
CUBE = (2, 4, 4, 4)


def iota(dim, *shape):
    return lax.broadcasted_iota(jnp.int32, shape, dim)


def onehot(mask):
    return jnp.where(mask, 1.0, 0.0).astype(jnp.bfloat16)


def cols(p):
    return pl.ds(COLS[p][0], COLS[p][1])


def half(p, side):
    lo, n = COLS[p]
    return pl.ds(lo + SPLIT, n - SPLIT) if side else pl.ds(lo, SPLIT)


def place(p, v, w, dc, ref):
    if p == 0:
        return ref.at[dc, w, v, :, :, cols(0)]
    if p == 1:
        return ref.at[dc, v, :, w, :, cols(1)]
    return ref.at[dc, :, w, v, :, cols(2)]


def kernel(idx_hbm, gates_hbm, tok_hbm, wg_hbm, wu_hbm, wd_hbm, out_ref,
           idx_ref, gates_ref, tok_ref, wg, wu, wd, toka, idxa, gata, bld, mid, rbuf, ybuf, rmid, rbld,
           gxs, psum, phalf, pfin, acc, hbuf,
           wsem, ssem, isem, gsem, tsem, bsem, csem, cback, bback, hsem, fsem):
    c = lax.axis_index('ep2')
    e = lax.axis_index('ep')
    me = (e % 4, (e // 4) % 4, e // 16)
    bf = jnp.bfloat16
    f32 = jnp.float32

    def to(axis, off, dc):
        p = list(me)
        if axis is not None:
            p[axis] = (p[axis] + off) % 4
        return (0, (c + dc) % 2, p[2] * 16 + p[1] * 4 + p[0])

    small = [pltpu.make_async_copy(a, b, wsem.at[i]) for i, (a, b) in enumerate(
        ((idx_hbm, idx_ref), (tok_hbm, tok_ref), (gates_hbm, gates_ref)))]
    cps = [pltpu.make_async_copy(a, b, wsem.at[3 + i]) for i, (a, b) in enumerate(
        ((wg_hbm, wg), (wu_hbm, wu), (wd_hbm, wd)))]
    for q in small:
        q.start()
    bar = pltpu.get_barrier_semaphore()

    def sig(k, carry):
        for axis in AXES:
            for dc in CORES:
                pl.semaphore_signal(bar, inc=1, device_id=to(axis, k, dc), device_id_type=MESH)
        return carry

    lax.fori_loop(1, 4, sig, 0)
    pl.semaphore_signal(bar, inc=1, device_id=to(None, 0, 1), device_id_type=MESH)

    before = onehot(iota(0, T, T) < iota(1, T, T))
    widen = onehot((iota(0, 256, 32) >> 3) == iota(1, 256, 32))

    def select(idx8, g8, p, a):
        k = iota(0, 32, T)
        b, d = (p + 1) % 3, (p + 2) % 3
        want = (((c + (k >> 4)) & 1) * 64 + me[p] * WEIGHT[p] + ((me[b] + (k >> 2)) & 3) * WEIGHT[b]
                + ((me[d] + k) & 3) * WEIGHT[d])
        m = jnp.zeros(want.shape, f32)
        g = m
        for j in range(8):
            hit = idx8[j:j + 1, :] == want
            m = jnp.where(hit, 1.0, m)
            g = jnp.where(hit, g8[j:j + 1, :], g)
        rank = jnp.dot(m.astype(bf), before, preferred_element_type=f32)
        rm = jnp.where(m > 0.5, rank + 1.0, 0.0).astype(bf)
        r = jnp.dot(widen, rm, preferred_element_type=f32)
        on = r == ((iota(0, 256, T) & 7) + 1).astype(f32)
        hi = g.astype(bf)
        r1 = g - hi.astype(f32)
        md = r1.astype(bf)
        lo = (r1 - md.astype(f32)).astype(bf)
        for i, part in enumerate((hi, md, lo)):
            gx = jnp.where(on, jnp.dot(widen, part, preferred_element_type=f32), 0.0)
            gxs[p, a, i * T:i * T + T, :] = jnp.swapaxes(gx, 0, 1).astype(bf)
        return onehot(on)

    def build(p, a):
        n = COLS[p][1]
        if a == 0:
            sel, src = select(idx_ref[...], gates_ref[...], p, a), tok_ref[:, cols(p)]
        else:
            sel, src = select(idxa[p, a - 1], gata[p, a - 1], p, a), toka[a - 1, :, cols(p)]
        rows = jnp.dot(sel, src, preferred_element_type=f32).astype(bf).reshape(2, 4, 4, 8, n)
        for dc in CORES:
            mid[dc, 0, a, :, :, cols(p)] = rows[dc, 0]
            for v in NEXT:
                bld[dc, v - 1, a, :, :, cols(p)] = rows[dc, v]

    def send(a, b, s, r, dest):
        pltpu.make_async_remote_copy(a, b, ssem.at[s], r, device_id=dest, device_id_type=MESH).start()

    def take(ref, sem):
        pltpu.make_async_remote_copy(ref, ref, ssem.at[0], sem, device_id=to(None, 0, 1), device_id_type=MESH).wait_recv()

    def gather_tokens():
        for u in NEXT:
            for p in AXES:
                send(idx_ref, idxa.at[p, u - 1], 0, isem.at[u - 1], to(p, u, 0))
                if u != 2:
                    send(tok_ref.at[:, cols(p)], toka.at[u - 1, :, cols(p)], 1, tsem.at[p, u - 1], to(p, u, 0))
                send(gates_ref, gata.at[p, u - 1], 2, gsem.at[u - 1], to(p, u, 0))

    def second(dc, a):
        for p in AXES:
            for v in NEXT:
                send(bld.at[dc, v - 1, a, :, :, cols(p)], mid.at[dc, v, a, :, :, cols(p)], 3, bsem.at[dc, p, v - 1],
                     to((p + 1) % 3, v, 0))

    def last(dc, v):
        for p in AXES:
            if v:
                take(mid.at[dc, v, :, :, :, cols(p)], bsem.at[dc, p, v - 1])
            for w in range(1 - dc, 4):
                send(mid.at[dc, v, :, w, :, cols(p)], place(p, v, w, dc, rbuf), 4 + dc, csem.at[dc, p],
                     to((p + 2) % 3 if w else None, w, dc))
            if dc == 0:
                place(p, v, 0, 0, rbuf)[...] = mid[0, v, :, 0, :, cols(p)]

    for q in small:
        q.wait()
    for p in AXES:
        build(p, 0)
    pl.semaphore_wait(bar, 19)
    for q in cps:
        q.start()
    gather_tokens()
    second(0, 0)
    for a in (1, 3):
        for p in AXES:
            take(toka.at[a - 1, :, cols(p)], tsem.at[p, a - 1])
            send(toka.at[a - 1, :, half(p, a // 2)], toka.at[1, :, half(p, a // 2)], 6, tsem.at[p, 1], to(p, a, 0))
    for a in NEXT:
        take(idxa.at[:, a - 1], isem.at[a - 1])
        take(gata.at[:, a - 1], gsem.at[a - 1])
        for p in AXES:
            if a == 2:
                take(toka.at[1, :, cols(p)], tsem.at[p, 1])
            build(p, a)
        second(0, a)
    last(0, 0)
    for a in (0, 1, 3):
        second(1, a)
    for v in NEXT:
        last(0, v)
    second(1, 2)
    for v in (0, *NEXT):
        last(1, v)
    for q in cps:
        q.wait()

    def ffn(dc, h):
        x = rbuf[dc, 2 * h:2 * h + 2].reshape(256, D)
        a = jnp.dot(x, wg[...], preferred_element_type=f32)
        b = jnp.dot(x, wu[...], preferred_element_type=f32)
        hbuf[...] = (a * jax.nn.sigmoid(a) * b).astype(bf)
        y = jnp.dot(hbuf[...], wd[...], preferred_element_type=f32).astype(bf)
        ybuf[dc, 2 * h:2 * h + 2] = y.reshape(2, 4, 4, 8, D)

    def first_back(dc, h):
        for v in (*NEXT, 0):
            for p in AXES:
                if p == 1 and v // 2 != h:
                    continue
                for w in range(4):
                    if p == 0 and w // 2 != h:
                        continue
                    part = pl.ds(2 * h, 2) if p == 2 else pl.ds(0, 4)
                    src = ybuf.at[dc, part, w, v, :, cols(p)] if p == 2 else place(p, v, w, dc, ybuf)
                    dst = rmid.at[dc, v, part, w, :, cols(p)]
                    if w or dc:
                        send(src, dst, 7 + dc, cback.at[dc, v, p], to((p + 2) % 3 if w else None, 4 - w, dc))
                    else:
                        dst[...] = src[...]

    def landed(dc, v):
        for p in AXES:
            take(rmid.at[dc, v, :, pl.ds(1 - dc, 3 + dc), :, cols(p)], cback.at[dc, v, p])

    def second_back(dc, v, a):
        for p in AXES:
            send(rmid.at[dc, v, a, :, :, cols(p)], rbld.at[dc, v, a, :, :, cols(p)], 9, bback.at[a, p],
                 to((p + 1) % 3, 4 - v, 0))

    def mix(p, a):
        take(rbld.at[:, pl.ds(1, 3), a, :, :, cols(p)], bback.at[a, p])
        y = rbld[:, :, a, :, :, cols(p)].reshape(256, COLS[p][1])
        s = jnp.dot(gxs[p, a], y, preferred_element_type=f32)
        return s[:T] + s[T:2 * T] + s[2 * T:]

    take(rbuf.at[0, 1:4, :, :, :, cols(0)], csem.at[0, 0])
    take(rbuf.at[0, :, :, 1:4, :, cols(1)], csem.at[0, 1])
    take(rbuf.at[0, :, 1:4, :, :, cols(2)], csem.at[0, 2])
    ffn(0, 0)
    first_back(0, 0)
    ffn(0, 1)
    first_back(0, 1)
    for p in AXES:
        take(rbuf.at[1, :, :, :, :, cols(p)], csem.at[1, p])
    ffn(1, 0)
    first_back(1, 0)
    ffn(1, 1)
    first_back(1, 1)
    for v in NEXT:
        landed(0, v)
        second_back(0, v, 2)
    for a in (1, 3):
        for v in NEXT:
            second_back(0, v, a)
    for v in NEXT:
        landed(1, v)
        second_back(1, v, 2)
    for a in (1, 3):
        for v in NEXT:
            second_back(1, v, a)
    for dc in CORES:
        for v in NEXT:
            second_back(dc, v, 0)
    landed(0, 0)
    landed(1, 0)
    for dc in CORES:
        rbld[dc, 0] = rmid[dc, 0]

    for p in AXES:
        psum[1, :, cols(p)] = mix(p, 2)
    for p in AXES:
        for side in CORES:
            send(psum.at[1, :, half(p, side)], phalf.at[:, half(p, side)], 10, hsem.at[p, side], to(p, 1 if side else 3, 0))
    def total(p, side, part):
        a = 2 * side + 1
        send(psum.at[a - 1, :, half(p, part)], pfin.at[side, :, half(p, part)], 11, fsem.at[side, p], to(p, 4 - a, 0))

    for side in CORES:
        for p in AXES:
            psum[2 * side, :, cols(p)] = mix(p, 2 * side + 1)
        for p in AXES:
            total(p, side, 1 - side)
    for side in CORES:
        for p in AXES:
            take(phalf.at[:, half(p, side)], hsem.at[p, side])
            psum[2 * side, :, half(p, side)] += phalf[:, half(p, side)]
        for p in AXES:
            total(p, side, side)
    for p in AXES:
        acc[:, cols(p)] = tok_ref[:, cols(p)].astype(f32) + mix(p, 0)
    for side in CORES:
        for p in AXES:
            take(pfin.at[side, :, cols(p)], fsem.at[side, p])
            if side:
                out_ref[:, cols(p)] = (acc[:, cols(p)] + pfin[side, :, cols(p)]).astype(bf)
            else:
                acc[:, cols(p)] += pfin[side, :, cols(p)]

    for i, ref in enumerate((idxa, toka.at[0:2], gata, bld, mid.at[0, :, :, 1:4], mid.at[1], toka.at[0],
                             rmid.at[0, :, :, 1:4], rmid.at[1], rbld.at[:, 1:4], phalf, pfin)):
        take(ref, ssem.at[i])


def solution(mesh):
    row_spec = P(('dp', 'ep2', 'ep'), None)
    weight_spec = P(('ep2', 'ep'), None, None)

    def local_step(tokens, expert_idx, gates, w_gate, w_up, w_down):
        bf, i32, f32 = jnp.bfloat16, jnp.int32, jnp.float32
        dma = pltpu.SemaphoreType.DMA

        def vmem(*shape, dtype=bf):
            return pltpu.VMEM(shape, dtype)

        def rows(*shape):
            return vmem(*shape, 8, D)

        return pl.pallas_call(
            kernel,
            out_shape=jax.ShapeDtypeStruct((T, D), bf),
            in_specs=[pl.BlockSpec(memory_space=pl.ANY)] * 6,
            out_specs=pl.BlockSpec(memory_space=pltpu.VMEM),
            scratch_shapes=[
                vmem(8, T, dtype=i32), vmem(8, T, dtype=f32), vmem(T, D), vmem(D, F), vmem(D, F), vmem(F, D),
                vmem(3, T, D), vmem(3, 3, 8, T, dtype=i32), vmem(3, 3, 8, T, dtype=f32), rows(2, 3, 4, 4),
                *[rows(*CUBE) for _ in range(5)],
                vmem(3, 4, 3 * T, 256), vmem(3, T, D, dtype=f32), vmem(T, D, dtype=f32), vmem(2, T, D, dtype=f32),
                vmem(T, D, dtype=f32), vmem(256, F),
                *[dma(n) for n in ((6,), (12,), (3,), (3,), (3, 3), (2, 3, 3), (2, 3), (2, 4, 3), (4, 3), (3, 2), (2, 3))],
            ],
            compiler_params=pltpu.CompilerParams(collective_id=0, has_side_effects=True, vmem_limit_bytes=62 << 20),
        )(expert_idx.T, gates.T, tokens, w_gate[0], w_up[0], w_down[0])

    return jax.shard_map(local_step, mesh=mesh, in_specs=(row_spec, row_spec, row_spec, weight_spec, weight_spec, weight_spec),
                         out_specs=row_spec, check_vma=False)
```

time: 229 us -> 93.2 us (0.41)
  Pallas kernels: 0 us -> 91.1 us
  blocking collectives: 86.9 us -> 0 us
  waiting for transfers between devices: 61 us -> 0 us
  local copies, waits for them, and re-layouts: 34.6 us -> 1.88 us
  other arithmetic: 20.1 us -> 0 us
  matrix products: 17.5 us -> 0 us
  starting transfers between devices: 8.34 us -> 0 us
    pallas_call x0 -> x1, Pallas kernels: none -> 91.1 us  [local_step(): pl.pallas_call(kernel, out_shape=jax.ShapeDtypeStruct((T, D), bf), in_spe...]
    all_to_all x3 -> x0, blocking collectives: 86.9 us -> none  [the longest x1 71.4 us: local_step(): received = lax.all_to_all(send_buf, 'ep', 1, 1, tiled=True)]
    all_to_all x1 -> x0, waiting for transfers between devices: 61 us -> none  [local_step(): returned = lax.all_to_all(returned, 'ep', 1, 1, tiled=True)]
    gather x2 -> x0, local copies, waits for them, and re-layouts: 21.5 us -> none  [the longest x1 11.6 us: local_step(): jnp.take(returned.reshape(n_slots, d_model), slot_ids, axis=0)]
    dot_general x2 -> x0, matrix products: 17.5 us -> none  [the longest x1 12.3 us: local_step(): jnp.einsum('abecf,efd->abecd', inner_act, w_down, preferred_element_type=...]
    all_to_all x1 -> x0, starting transfers between devices: 8.34 us -> none  [local_step(): returned = lax.all_to_all(returned, 'ep', 1, 1, tiled=True)]
    scatter-add x1 -> x0, other arithmetic: 7.62 us -> none  [local_step(): jax.ops.segment_sum(token_of - tok_rows, slot_ids, num_segments=n_slots)]
    all_to_all x3 -> x0, local copies, waits for them, and re-layouts: 7.6 us -> none  [the longest x1 4.74 us: local_step(): returned = lax.all_to_all(returned, 'ep', 1, 1, tiled=True)]
  transfers between devices with their start and end apart: 1 -> 0, of which waited for: 1 -> 0; matrix products, arithmetic and copies ran while one was open for 0% -> 0% of each run, Pallas kernels for 0% -> 0%
where the time goes in v5:
time: 93.2 us; the launch traced here: 93 us
  Pallas kernels  91.1 us (98%)
  local copies, waits for them, and re-layouts  1.88 us (2%)
    pallas_call x1, Pallas kernels, local_step(): pl.pallas_call(kernel, out_shape=jax.ShapeDtypeStruct((T, D), bf), in_spe...  91.1 us
    unnamed x1, local copies, waits for them, and re-layouts  1.88 us

profile of v5, /device:TPU:1, one launch (start us, length us, event | category | flops | bytes accessed | tf_op | source)
XLA Modules:
  0.0 93.0 jit_solution(6919583123846791682)
XLA Ops:
  0.0 91.1 %shard_map.64 = bf16[128,2048]{1,0:T(8,128)(2,1)} custom-call(s32[8,128]{1,0:T(8,128)} %bitcast.8, f32[8,128]{1,0:T(8,128)} %bitcast.9, bf16[128,2048]{1,0:T(8,128)(2,1)} %tok_hbm.1, bf16[2048,768]{1,0:T(8,128)(2,1)} %bitcast.5, bf16[2048,768]{1,0:T(8,128)(2,1)} %bitcast.6, bf16[768,2048]{1,0:T(8,128)(2,1)} %bitcast.7), custom_call_target="tpu_custom_call" | custom-call | tf_op jit(solution)/shard_map/pallas_call | solution.py:301
  91.1 1.9 %copy.8 = bf16[128,2048]{1,0:T(8,128)(2,1)} copy(bf16[128,2048]{1,0:T(8,128)(2,1)} %shard_map.64) | data formatting | bytes 1048576

commit v6 on v5

--- a/solution.py
+++ b/solution.py
@@ -12,7 +12,7 @@
 AXES = range(3)
 CORES = range(2)
 NEXT = (1, 3, 2)
-COLS = ((0, 768), (768, 640), (1408, 640))
+COLS = ((0, 640), (640, 640), (1280, 768))
 SPLIT = 384
 WEIGHT = (1, 4, 16)
 CUBE = (2, 4, 4, 4)
@@ -154,6 +154,7 @@
         q.start()
     gather_tokens()
     second(0, 0)
+    second(1, 0)
     for a in (1, 3):
         for p in AXES:
             take(toka.at[a - 1, :, cols(p)], tsem.at[p, a - 1])
@@ -167,7 +168,7 @@
             build(p, a)
         second(0, a)
     last(0, 0)
-    for a in (0, 1, 3):
+    for a in (1, 3):
         second(1, a)
     for v in NEXT:
         last(0, v)
@@ -220,8 +221,8 @@
     take(rbuf.at[0, :, :, 1:4, :, cols(1)], csem.at[0, 1])
     take(rbuf.at[0, :, 1:4, :, :, cols(2)], csem.at[0, 2])
     ffn(0, 0)
+    ffn(0, 1)
     first_back(0, 0)
-    ffn(0, 1)
     first_back(0, 1)
     for p in AXES:
         take(rbuf.at[1, :, :, :, :, cols(p)], csem.at[1, p])

time: 93.2 us -> 92.1 us (0.988)
  Pallas kernels: 91.1 us -> 89.5 us
    pallas_call x1, Pallas kernels: 91.1 us -> 89.5 us  [local_step(): pl.pallas_call(kernel, out_shape=jax.ShapeDtypeStruct((T, D), bf), in_spe...]
where the time goes in v6:
time: 92.1 us; the launch traced here: 91.4 us
  Pallas kernels  89.5 us (97%)
  local copies, waits for them, and re-layouts  1.88 us (2%)
    pallas_call x1, Pallas kernels, local_step(): pl.pallas_call(kernel, out_shape=jax.ShapeDtypeStruct((T, D), bf), in_spe...  89.5 us
    unnamed x1, local copies, waits for them, and re-layouts  1.88 us

profile of v6, /device:TPU:1, one launch (start us, length us, event | category | flops | bytes accessed | tf_op | source)
XLA Modules:
  0.0 91.4 jit_solution(4473269771072506545)
XLA Ops:
  0.0 89.5 %shard_map.64 = bf16[128,2048]{1,0:T(8,128)(2,1)} custom-call(s32[8,128]{1,0:T(8,128)} %bitcast.8, f32[8,128]{1,0:T(8,128)} %bitcast.9, bf16[128,2048]{1,0:T(8,128)(2,1)} %tok_hbm.1, bf16[2048,768]{1,0:T(8,128)(2,1)} %bitcast.5, bf16[2048,768]{1,0:T(8,128)(2,1)} %bitcast.6, bf16[768,2048]{1,0:T(8,128)(2,1)} %bitcast.7), custom_call_target="tpu_custom_call" | custom-call | tf_op jit(solution)/shard_map/pallas_call | solution.py:302
  89.5 1.9 %copy.8 = bf16[128,2048]{1,0:T(8,128)(2,1)} copy(bf16[128,2048]{1,0:T(8,128)(2,1)} %shard_map.64) | data formatting | bytes 1048576

commit v7 on v6

--- a/solution.py
+++ b/solution.py
@@ -198,21 +198,21 @@
                     src = ybuf.at[dc, part, w, v, :, cols(p)] if p == 2 else place(p, v, w, dc, ybuf)
                     dst = rmid.at[dc, v, part, w, :, cols(p)]
                     if w or dc:
-                        send(src, dst, 7 + dc, cback.at[dc, v, p], to((p + 2) % 3 if w else None, 4 - w, dc))
+                        send(src, dst, 7 + dc, cback.at[dc, v], to((p + 2) % 3 if w else None, 4 - w, dc))
                     else:
                         dst[...] = src[...]
 
     def landed(dc, v):
-        for p in AXES:
-            take(rmid.at[dc, v, :, pl.ds(1 - dc, 3 + dc), :, cols(p)], cback.at[dc, v, p])
+        take(rmid.at[dc, v, :, pl.ds(1 - dc, 3 + dc)], cback.at[dc, v])
 
     def second_back(dc, v, a):
         for p in AXES:
-            send(rmid.at[dc, v, a, :, :, cols(p)], rbld.at[dc, v, a, :, :, cols(p)], 9, bback.at[a, p],
+            send(rmid.at[dc, v, a, :, :, cols(p)], rbld.at[dc, v, a, :, :, cols(p)], 9, bback.at[a],
                  to((p + 1) % 3, 4 - v, 0))
 
     def mix(p, a):
-        take(rbld.at[:, pl.ds(1, 3), a, :, :, cols(p)], bback.at[a, p])
+        if p == 0:
+            take(rbld.at[:, pl.ds(1, 3), a], bback.at[a])
         y = rbld[:, :, a, :, :, cols(p)].reshape(256, COLS[p][1])
         s = jnp.dot(gxs[p, a], y, preferred_element_type=f32)
         return s[:T] + s[T:2 * T] + s[2 * T:]
@@ -310,7 +310,7 @@
                 *[rows(*CUBE) for _ in range(5)],
                 vmem(3, 4, 3 * T, 256), vmem(3, T, D, dtype=f32), vmem(T, D, dtype=f32), vmem(2, T, D, dtype=f32),
                 vmem(T, D, dtype=f32), vmem(256, F),
-                *[dma(n) for n in ((6,), (12,), (3,), (3,), (3, 3), (2, 3, 3), (2, 3), (2, 4, 3), (4, 3), (3, 2), (2, 3))],
+                *[dma(n) for n in ((6,), (12,), (3,), (3,), (3, 3), (2, 3, 3), (2, 3), (2, 4), (4,), (3, 2), (2, 3))],
             ],
             compiler_params=pltpu.CompilerParams(collective_id=0, has_side_effects=True, vmem_limit_bytes=62 << 20),
         )(expert_idx.T, gates.T, tokens, w_gate[0], w_up[0], w_down[0])

time: 92.1 us -> 91.9 us (level)
  no operation moved by 1% of the time
where the time goes in v7:
time: 91.9 us; the launch traced here: 91.2 us
  Pallas kernels  89.3 us (97%)
  local copies, waits for them, and re-layouts  1.88 us (2%)
    pallas_call x1, Pallas kernels, local_step(): pl.pallas_call(kernel, out_shape=jax.ShapeDtypeStruct((T, D), bf), in_spe...  89.3 us
    unnamed x1, local copies, waits for them, and re-layouts  1.88 us

profile of v7, /device:TPU:1, one launch (start us, length us, event | category | flops | bytes accessed | tf_op | source)
XLA Modules:
  0.0 91.2 jit_solution(16982423260890702860)
XLA Ops:
  0.0 89.3 %shard_map.64 = bf16[128,2048]{1,0:T(8,128)(2,1)} custom-call(s32[8,128]{1,0:T(8,128)} %bitcast.8, f32[8,128]{1,0:T(8,128)} %bitcast.9, bf16[128,2048]{1,0:T(8,128)(2,1)} %tok_hbm.1, bf16[2048,768]{1,0:T(8,128)(2,1)} %bitcast.5, bf16[2048,768]{1,0:T(8,128)(2,1)} %bitcast.6, bf16[768,2048]{1,0:T(8,128)(2,1)} %bitcast.7), custom_call_target="tpu_custom_call" | custom-call | tf_op jit(solution)/shard_map/pallas_call | solution.py:302
  89.3 1.9 %copy.8 = bf16[128,2048]{1,0:T(8,128)(2,1)} copy(bf16[128,2048]{1,0:T(8,128)(2,1)} %shard_map.64) | data formatting | bytes 1048576
